TPU v7x, 32 devices: a whole 2x2x4 slice. The times are simulated.
32 devices in a mesh: gz: 8 (over z, x), gy: 4 (over y, core).
Axes of the slice: x: 2, y: 2, z: 4, core: 2. Of those that a mesh axis runs over, the one named last changes fastest.
Arguments:
- populations: float32 [19, 24, 192, 128], P(None, 'gz', 'gy'), may hold values from 0.1 to 25, as said below
- solute: float32 [7, 24, 192, 128], P(None, 'gz', 'gy'), may hold values from 0.05 to 3, as said below
- pore_mask: int32 [24, 192, 128], P('gz', 'gy'), may hold values from 0 to 2
- mineral_ids: int32 [24, 192, 128], P('gz', 'gy'), may hold values from 0 to 7
- reaction_rates: float32 [8], replicated, may hold values from 0.05 to 0.6
- saturation: float32 [8], replicated, may hold values from 0.5 to 6
Outputs:
- flow_next: float32 [19, 24, 192, 128], P(None, 'gz', 'gy')
- solute_next: float32 [7, 24, 192, 128], P(None, 'gz', 'gy')
Inputs may be any that keep to these rules, and one draw needn't show every extreme that they name: `populations`: every population is positive. `solute`: every population is positive.
All inputs are finite; a program needn't handle non-finite values.
Results may differ from a plain program's by a relative error of at most 0.0003.
Values sent between devices are 32-bit elements; how exact they have to be, the bound alone decides.
A program may use at most 64 MiB of HBM per device.

v0:
```python
import jax
import jax.numpy as jnp
import numpy as np
from jax import lax
from jax.sharding import PartitionSpec as P

LINKS19 = np.array(
    [
        [0, 0, 0],
        [1, 0, 0],
        [-1, 0, 0],
        [0, 1, 0],
        [0, -1, 0],
        [0, 0, 1],
        [0, 0, -1],
        [1, 1, 0],
        [-1, -1, 0],
        [1, -1, 0],
        [-1, 1, 0],
        [1, 0, 1],
        [-1, 0, -1],
        [1, 0, -1],
        [-1, 0, 1],
        [0, 1, 1],
        [0, -1, -1],
        [0, 1, -1],
        [0, -1, 1],
    ]
)
REVERSE19 = [0, 2, 1, 4, 3, 6, 5, 8, 7, 10, 9, 12, 11, 14, 13, 16, 15, 18, 17]
WEIGHTS19 = np.array([1.0 / 3.0] + [1.0 / 18.0] * 6 + [1.0 / 36.0] * 12)
WEIGHTS7 = np.array([0.25] + [0.125] * 6)
RELAX_FLOW = 1.25
RELAX_SOLUTE = 1.4


def with_halo(cells, sides, width):
    for axis, dim in sides:
        count = lax.axis_size(axis)
        head = lax.slice_in_dim(cells, 0, width, axis=dim)
        tail = lax.slice_in_dim(cells, cells.shape[dim] - width, cells.shape[dim], axis=dim)
        cells = jnp.concatenate(
            [
                lax.ppermute(tail, axis, [(i, (i + 1) % count) for i in range(count)]),
                cells,
                lax.ppermute(head, axis, [((i + 1) % count, i) for i in range(count)]),
            ],
            axis=dim,
        )
    return cells


def passed_along(shard, axis, by):
    count = lax.axis_size(axis)
    return lax.ppermute(shard, axis, [(i, (i + by) % count) for i in range(count)])


def shifted(block, axis, distance):
    devices = range(lax.axis_size(axis))
    route = [(i - distance, i) for i in devices if i - distance in devices]
    return lax.ppermute(block, axis, route)


def moment(values, lattice):
    link_table = jnp.asarray(lattice, jnp.float32)
    return jnp.tensordot(link_table.T, values, axes=1, precision=lax.Precision.HIGHEST)


def equilibrium(density, velocity, lattice, weights, linear, quadratic, square_term):
    link_table = jnp.asarray(lattice, jnp.float32)
    projected = jnp.tensordot(link_table, velocity, axes=1, precision=lax.Precision.HIGHEST)
    speed = jnp.sum(velocity * velocity, 0)
    scaled = jnp.asarray(weights, jnp.float32)[:, None, None, None]
    return (
        scaled
        * density
        * (1.0 + linear * projected + quadratic * projected * projected - square_term * speed)
    )


def lookup(mineral_ids, values_table):
    kinds = jnp.arange(values_table.shape[0], dtype=jnp.int32)[:, None, None, None]
    return jnp.sum(jnp.where(mineral_ids[None] == kinds, values_table[:, None, None, None], 0.0), 0)


def neighbour(padded, shift_z, shift_y, shift_x, depth_cells, width_cells):
    window = lax.slice_in_dim(padded, 1 - shift_z, 1 - shift_z + depth_cells, axis=0)
    window = lax.slice_in_dim(window, 1 - shift_y, 1 - shift_y + width_cells, axis=1)
    return jnp.roll(window, shift_x, axis=2)


def on_device(populations, solute, pore_mask, mineral_ids, reaction_rates, saturation):
    depth_cells, width_cells = (pore_mask.shape[0], pore_mask.shape[1])
    mask_cycle = with_halo(pore_mask, (("gz", 0), ("gy", 1)), 1)
    row_index = lax.axis_index("gy")
    row_total = lax.axis_size("gy")
    row_ids = lax.broadcasted_iota(jnp.int32, mask_cycle.shape, 1)
    walled = (row_ids == 0) & (row_index == 0) | (row_ids == width_cells + 1) & (
        row_index == row_total - 1
    )
    mask_cycle = jnp.where(walled, 0, mask_cycle)
    sources = []
    for direction in range(19):
        shift_z, shift_y, shift_x = (int(v) for v in LINKS19[direction])
        sources.append(neighbour(mask_cycle, shift_z, shift_y, shift_x, depth_cells, width_cells))
    density = jnp.sum(populations, 0)
    velocity = moment(populations, LINKS19) / density
    balanced = equilibrium(density, velocity, LINKS19, WEIGHTS19, 3.0, 4.5, 1.5)
    relaxed = populations - (populations - balanced) / RELAX_FLOW
    arrived = []
    rising = [d for d in range(19) if LINKS19[d][0] == 1]
    falling = [d for d in range(19) if LINKS19[d][0] == -1]
    lower_planes = passed_along(jnp.stack([relaxed[d, depth_cells - 1 :] for d in rising]), "gz", 1)
    upper_planes = passed_along(jnp.stack([relaxed[d, :1] for d in falling]), "gz", -1)
    after_depth = []
    for direction in range(19):
        if direction in rising:
            after_depth.append(
                jnp.concatenate([lower_planes[rising.index(direction)], relaxed[direction, :-1]], 0)
            )
        elif direction in falling:
            after_depth.append(
                jnp.concatenate([relaxed[direction, 1:], upper_planes[falling.index(direction)]], 0)
            )
        else:
            after_depth.append(relaxed[direction])
    across_up = [d for d in range(19) if LINKS19[d][1] == 1]
    across_down = [d for d in range(19) if LINKS19[d][1] == -1]
    lower_rows = shifted(
        jnp.stack([after_depth[d][:, width_cells - 1 :] for d in across_up]), "gy", 1
    )
    upper_rows = shifted(jnp.stack([after_depth[d][:, :1] for d in across_down]), "gy", -1)
    for direction in range(19):
        if direction in across_up:
            moved = jnp.concatenate(
                [lower_rows[across_up.index(direction)], after_depth[direction][:, :-1]], 1
            )
        elif direction in across_down:
            moved = jnp.concatenate(
                [after_depth[direction][:, 1:], upper_rows[across_down.index(direction)]], 1
            )
        else:
            moved = after_depth[direction]
        arrived.append(jnp.roll(moved, int(LINKS19[direction][2]), axis=2))
    passed = jnp.stack(
        [jnp.where(sources[d] == 0, relaxed[REVERSE19[d]], arrived[d]) for d in range(19)]
    )
    flow_next = jnp.where(pore_mask[None] == 0, populations, passed)
    density_next = jnp.sum(flow_next, 0)
    velocity_next = jnp.where(pore_mask[None] > 0, moment(flow_next, LINKS19) / density_next, 0.0)
    concentration = jnp.sum(solute, 0)
    rate_cell = lookup(mineral_ids, reaction_rates)
    target = lookup(mineral_ids, saturation)
    reaction = jnp.where(pore_mask == 2, -rate_cell * (concentration - target), 0.0)
    solute_balanced = equilibrium(
        concentration, velocity_next, LINKS19[:7], WEIGHTS7, 4.0, 0.0, 0.0
    )
    weights = jnp.asarray(WEIGHTS7, jnp.float32)[:, None, None, None]
    solute_relaxed = solute - (solute - solute_balanced) / RELAX_SOLUTE + weights * reaction
    solute_pulled = []
    solute_padded = with_halo(solute_relaxed, (("gz", 1), ("gy", 2)), 1)
    for direction in range(7):
        shift_z, shift_y, shift_x = (int(v) for v in LINKS19[direction])
        solute_pulled.append(
            neighbour(solute_padded[direction], shift_z, shift_y, shift_x, depth_cells, width_cells)
        )
    solute_moved = [
        jnp.where(sources[d] == 0, solute_relaxed[REVERSE19[d]], solute_pulled[d]) for d in range(7)
    ]
    solute_next = jnp.where(pore_mask[None] == 0, solute, jnp.stack(solute_moved))
    return (flow_next, solute_next)


def solution(mesh):
    return jax.shard_map(
        on_device,
        mesh=mesh,
        in_specs=(
            P(None, "gz", "gy", None),
            P(None, "gz", "gy", None),
            P("gz", "gy", None),
            P("gz", "gy", None),
            P(),
            P(),
        ),
        out_specs=(P(None, "gz", "gy", None), P(None, "gz", "gy", None)),
        check_vma=False,
    )
```

profile of v0, /device:TPU:0, one launch (start us, length us, event | category | flops | bytes accessed | tf_op | source)
XLA Modules:
  0.0 58.8 jit_solution(13145331232652178926)
XLA Ops:
  0.7 1.5 %reduce_sum.63 = f32[3,48,128]{2,1,0:T(8,128)S(1)} reduce(f32[19,3,48,128]{3,2,1,0:T(8,128)} %param.13, f32[]{:T(128)} %constant.18.clone.1), dimensions={0}, to_apply=%region_0.1 | reduce | flops 331776 | bytes 1474564 | tf_op jit(solution)/shard_map/reduce_sum | solution.py:106
  2.4 1.5 %multiply_reduce_fusion.1 = (f32[3,48,128]{2,1,0:T(8,128)S(1)}, f32[3,3,48,128]{3,0,2,1:T(4,128)S(1)}) fusion(f32[3,48,128]{2,1,0:T(8,128)S(1)} %reduce_sum.63, f32[19,3,1,1]{0,1,3,2:T(4,128)S(1)} %copy-done.16, f32[19,3,48,128]{3,2,1,0:T(8,128)S(1)} %copy-done), kind=kOutput, calls=%fused_computation.28 | convolution fusion | flops 12754944 | bytes 1769700 | tf_op jit(solution)/shard_map/dot_general | solution.py:66
  4.0 1.6 %fusion.65 = f32[19,3,48,128]{3,0,2,1:T(8,128)S(1)} fusion(f32[19,3,1,1]{0,1,3,2:T(4,128)S(1)} %copy-done.16, f32[3,3,48,128]{3,0,2,1:T(4,128)S(1)} %get-tuple-element.107), kind=kOutput, calls=%fused_computation.280 | convolution fusion | flops 12607488 | bytes 1622244 | tf_op jit(solution)/shard_map/dot_general | solution.py:71
  9.3 3.0 %collective-permute-start.4 = (f32[5,1,48,128]{3,2,1,0:T(8,128)}, f32[5,1,48,128]{3,2,1,0:T(8,128)}, u32[]{:S(2)}, u32[]{:S(2)}) collective-permute-start(f32[5,1,48,128]{3,2,1,0:T(8,128)} %get-tuple-element.41), channel_id=1, source_target_pairs={{0,4},{4,8},{8,12},{12,16},{16,20},{20,24},{24,28},{28,0},{1,5},{5... | collective-permute-start | bytes 368648 | tf_op jit(solution)/shard_map/ppermute | solution.py:55
  12.9 1.5 %collective-permute-start = (s32[1,48,128]{2,1,0:T(8,128)}, s32[1,48,128]{2,1,0:T(8,128)}, u32[]{:S(2)}, u32[]{:S(2)}) collective-permute-start(s32[1,48,128]{2,1,0:T(8,128)} %get-tuple-element.95), channel_id=1, source_target_pairs={{0,4},{4,8},{8,12},{12,16},{16,20},{20,24},{24,28},{28,0},{1,5},{5... | collective-permute-start | bytes 73736 | tf_op jit(solution)/shard_map/ppermute | solution.py:44
  14.5 3.2 %collective-permute-start.1 = (s32[1,48,128]{2,1,0:T(8,128)}, s32[1,48,128]{2,1,0:T(8,128)}, u32[]{:S(2)}, u32[]{:S(2)}) collective-permute-start(s32[1,48,128]{2,1,0:T(8,128)} %get-tuple-element.94), channel_id=1, source_target_pairs={{4,0},{8,4},{12,8},{16,12},{20,16},{24,20},{28,24},{0,28},{5,1},{9... | collective-permute-start | bytes 73736 | tf_op jit(solution)/shard_map/ppermute | solution.py:46
  18.6 0.8 %slice_bitcast_fusion.47 = (f32[2,48,128]{2,1,0:T(8,128)}, f32[2,48,128]{2,1,0:T(8,128)S(1)}, f32[2,48,128]{2,1,0:T(8,128)}, f32[2,48,128]{2,1,0:T(8,128)}, f32[...) fusion(f32[19,3,48,128]{3,2,1,0:T(8,128)S(1)} %fusion.9), kind=kLoop, calls=%fused_computation.228 | loop fusion | bytes 983040 | tf_op jit(solution)/shard_map/squeeze | solution.py:123
  19.5 1.1 %select_reduce_fusion.1 = (f32[3,48,128]{2,1,0:T(8,128)S(1)}, f32[3,48,128]{2,1,0:T(8,128)S(1)}) fusion(f32[8]{0:T(128)S(1)} %copy-done.18, s32[3,48,128]{2,1,0:T(8,128)} %param.16, f32[8]{0:T(128)S(1)} %copy-done.19), kind=kLoop, calls=%fused_computation.18 | loop fusion | flops 700416 | bytes 221248 | tf_op jit(solution)/shard_map/reduce_sum | solution.py:83
  23.4 0.9 %collective-permute-done.3 = s32[5,1,128]{2,1,0:T(1,128)S(1)} collective-permute-done((s32[5,1,128]{2,1,0:T(1,128)S(1)}, s32[5,1,128]{2,1,0:T(1,128)S(1)}, u32[]{:S(2)}, u32[]{:S(2)}) %collective-permute-start.3) | collective-permute-done | bytes 2592 | tf_op jit(solution)/shard_map/ppermute | solution.py:46
  24.3 1.7 %collective-permute-done.2 = s32[5,1,128]{2,1,0:T(1,128)S(1)} collective-permute-done((s32[5,1,128]{2,1,0:T(1,128)S(1)}, s32[5,1,128]{2,1,0:T(1,128)S(1)}, u32[]{:S(2)}, u32[]{:S(2)}) %collective-permute-start.2) | collective-permute-done | bytes 2592 | tf_op jit(solution)/shard_map/ppermute | solution.py:44
  26.5 0.9 %slice_bitcast_fusion.58 = (f32[1,48,128]{2,1,0:T(8,128)S(1)}, f32[1,48,128]{2,1,0:T(8,128)S(1)}, f32[1,48,128]{2,1,0:T(8,128)S(1)}, f32[1,48,128]{2,1,0:T(8,128)S(1)}, f32[1,48,128]{2,1,0:T(8,128)S(1)}) fusion(f32[5,1,48,128]{3,2,1,0:T(8,128)} %collective-permute-done.4), kind=kLoop, calls=%fused_computation.243 | loop fusion | bytes 245760 | tf_op jit(solution)/shard_map/squeeze | solution.py:119
  27.6 0.8 %slice_bitcast_fusion.57 = (f32[1,48,128]{2,1,0:T(8,128)S(1)}, f32[1,48,128]{2,1,0:T(8,128)S(1)}, f32[1,48,128]{2,1,0:T(8,128)S(1)}, f32[1,48,128]{2,1,0:T(8,128)S(1)}, f32[1,48,128]{2,1,0:T(8,128)S(1)}) fusion(f32[5,1,48,128]{3,2,1,0:T(8,128)} %collective-permute-done.5), kind=kLoop, calls=%fused_computation.242 | loop fusion | bytes 245760 | tf_op jit(solution)/shard_map/squeeze | solution.py:123
  28.8 2.0 %collective-permute-start.6 = (f32[5,3,1,128]{3,2,1,0:T(1,128)S(1)}, f32[5,3,1,128]{3,2,1,0:T(1,128)S(1)}, u32[]{:S(2)}, u32[]{:S(2)}) collective-permute-start(f32[5,3,1,128]{3,2,1,0:T(1,128)S(1)} %constant_dynamic-update-slice_fusion.13), channel_id=1, source_target_pairs={{0,1},{1,2},{2,3},{4,5},{5,6},{6,7},{8,9},{9,10},{10,11},{12,13},{... | collective-permute-start | bytes 23048 | tf_op jit(solution)/shard_map/ppermute | solution.py:61
  31.7 1.3 %collective-permute-start.7 = (f32[5,3,1,128]{3,2,1,0:T(1,128)S(1)}, f32[5,3,1,128]{3,2,1,0:T(1,128)S(1)}, u32[]{:S(2)}, u32[]{:S(2)}) collective-permute-start(f32[5,3,1,128]{3,2,1,0:T(1,128)S(1)} %constant_dynamic-update-slice_fusion.18), channel_id=1, source_target_pairs={{1,0},{2,1},{3,2},{5,4},{6,5},{7,6},{9,8},{10,9},{11,10},{13,12},{... | collective-permute-start | bytes 23048 | tf_op jit(solution)/shard_map/ppermute | solution.py:61
  33.2 2.6 %collective-permute-done.7 = f32[5,3,1,128]{3,2,1,0:T(1,128)S(1)} collective-permute-done((f32[5,3,1,128]{3,2,1,0:T(1,128)S(1)}, f32[5,3,1,128]{3,2,1,0:T(1,128)S(1)}, u32[]{:S(2)}, u32[]{:S(2)}) %collective-permute-start.7) | collective-permute-done | bytes 7712 | tf_op jit(solution)/shard_map/ppermute | solution.py:61
  38.3 1.9 %multiply_reduce_fusion = (f32[3,48,128]{2,1,0:T(8,128)S(1)}, f32[3,3,48,128]{3,0,2,1:T(4,128)S(1)}) fusion(f32[3,48,128]{2,1,0:T(8,128)S(1)} %get-tuple-element.6, f32[19,3,1,1]{0,1,3,2:T(4,128)S(1)} %copy-done.17, f32[19,3,48,128]{3,2,1,0:T(8,128)S(1)} %get-tuple-element.7, pred[3,48,128]{2,1,0:T(8,128)(4,1)S(1)} %get-tuple-element.92), kind=kOutput, calls=%fused_computation.27 | convolution fusion | flops 12810240 | bytes 1788132 | tf_op jit(solution)/shard_map/dot_general | solution.py:66
  40.2 0.8 %fusion.66 = f32[7,3,48,128]{3,0,2,1:T(8,128)S(1)} fusion(f32[7,3,1,1]{0,1,3,2:T(4,128)S(1)} %copy-done.15, f32[3,3,48,128]{3,0,2,1:T(4,128)S(1)} %get-tuple-element.109), kind=kOutput, calls=%fused_computation.281 | convolution fusion | flops 4644864 | bytes 737364 | tf_op jit(solution)/shard_map/dot_general | solution.py:71
  41.3 2.8 %collective-permute-start.9 = (f32[7,1,48,128]{3,2,1,0:T(8,128)S(1)}, f32[7,1,48,128]{3,2,1,0:T(8,128)S(1)}, u32[]{:S(2)}, u32[]{:S(2)}) collective-permute-start(f32[7,1,48,128]{3,2,1,0:T(8,128)S(1)} %get-tuple-element.59), channel_id=1, source_target_pairs={{4,0},{8,4},{12,8},{16,12},{20,16},{24,20},{28,24},{0,28},{5,1},{9... | collective-permute-start | bytes 516104 | tf_op jit(solution)/shard_map/ppermute | solution.py:46
  44.1 2.9 %collective-permute-done.9 = f32[7,1,48,128]{3,2,1,0:T(8,128)S(1)} collective-permute-done((f32[7,1,48,128]{3,2,1,0:T(8,128)S(1)}, f32[7,1,48,128]{3,2,1,0:T(8,128)S(1)}, u32[]{:S(2)}, u32[]{:S(2)}) %collective-permute-start.9) | collective-permute-done | bytes 172064 | tf_op jit(solution)/shard_map/ppermute | solution.py:46
  47.0 5.3 %collective-permute-done.8 = f32[7,1,48,128]{3,2,1,0:T(8,128)S(1)} collective-permute-done((f32[7,1,48,128]{3,2,1,0:T(8,128)S(1)}, f32[7,1,48,128]{3,2,1,0:T(8,128)S(1)}, u32[]{:S(2)}, u32[]{:S(2)}) %collective-permute-start.8) | collective-permute-done | bytes 172064 | tf_op jit(solution)/shard_map/ppermute | solution.py:44
  52.3 1.8 %collective-permute-start.11 = (f32[7,5,1,128]{3,2,1,0:T(1,128)S(1)}, f32[7,5,1,128]{3,2,1,0:T(1,128)S(1)}, u32[]{:S(2)}, u32[]{:S(2)}) collective-permute-start(f32[7,5,1,128]{3,2,1,0:T(1,128)S(1)} %get-tuple-element.57), channel_id=1, source_target_pairs={{1,0},{2,1},{3,2},{0,3},{5,4},{6,5},{7,6},{4,7},{9,8},{10,9},{11,1... | collective-permute-start | bytes 53768 | tf_op jit(solution)/shard_map/ppermute | solution.py:46
  54.1 1.5 %collective-permute-done.11 = f32[7,5,1,128]{3,2,1,0:T(1,128)S(1)} collective-permute-done((f32[7,5,1,128]{3,2,1,0:T(1,128)S(1)}, f32[7,5,1,128]{3,2,1,0:T(1,128)S(1)}, u32[]{:S(2)}, u32[]{:S(2)}) %collective-permute-start.11) | collective-permute-done | bytes 17952 | tf_op jit(solution)/shard_map/ppermute | solution.py:46
  55.5 1.8 %collective-permute-done.10 = f32[7,5,1,128]{3,2,1,0:T(1,128)S(1)} collective-permute-done((f32[7,5,1,128]{3,2,1,0:T(1,128)S(1)}, f32[7,5,1,128]{3,2,1,0:T(1,128)S(1)}, u32[]{:S(2)}, u32[]{:S(2)}) %collective-permute-start.10) | collective-permute-done | bytes 17952 | tf_op jit(solution)/shard_map/ppermute | solution.py:44
  57.9 0.9 %broadcast_select_fusion.1 = f32[7,3,48,128]{3,2,1,0:T(8,128)} fusion(f32[7,3,48,128]{3,2,1,0:T(8,128)S(1)} %copy-done.1, f32[7,3,48,128]{3,2,1,0:T(8,128)S(1)} %constant_dynamic-update-slice_fusion.42, pred[3,48,128]{2,1,0:T(8,128)(4,1)S(1)} %get-tuple-element.93), kind=kLoop, calls=%fused_computation.29 | loop fusion | flops 129024 | bytes 1566720 | tf_op jit(solution)/shard_map/jit(_where)/select_n | solution.py:170
  (138 shorter events, 13.3 us)
Async XLA Ops:
  5.6 6.7 %copy-start.4 = (s32[3,48,128]{2,1,0:T(8,128)S(1)}, s32[3,48,128]{2,1,0:T(8,128)}, u32[]{:S(2)}) copy-start(s32[3,48,128]{2,1,0:T(8,128)} %param.15) | copy-start | bytes 221188
  6.2 13.2 %copy-start.1 = (f32[7,3,48,128]{3,2,1,0:T(8,128)S(1)}, f32[7,3,48,128]{3,2,1,0:T(8,128)}, u32[]{:S(2)}) copy-start(f32[7,3,48,128]{3,2,1,0:T(8,128)} %param.14) | copy-start | bytes 1548292
  6.2 13.2 %copy-start.18 = (f32[8]{0:T(128)S(1)}, f32[8]{0:T(128)}, u32[]{:S(2)}) copy-start(f32[8]{0:T(128)} %param.17) | copy-start | bytes 100
  6.2 13.2 %copy-start.19 = (f32[8]{0:T(128)S(1)}, f32[8]{0:T(128)}, u32[]{:S(2)}) copy-start(f32[8]{0:T(128)} %param.18) | copy-start | bytes 100
  9.3 17.1 %collective-permute-start.4 = (f32[5,1,48,128]{3,2,1,0:T(8,128)}, f32[5,1,48,128]{3,2,1,0:T(8,128)}, u32[]{:S(2)}, u32[]{:S(2)}) collective-permute-start(f32[5,1,48,128]{3,2,1,0:T(8,128)} %get-tuple-element.41), channel_id=1, source_target_pairs={{0,4},{4,8},{8,12},{12,16},{16,20},{20,24},{24,28},{28,0},{1,5},{5... | collective-permute-start | bytes 368648 | tf_op jit(solution)/shard_map/ppermute | solution.py:55
  12.9 8.3 %collective-permute-start = (s32[1,48,128]{2,1,0:T(8,128)}, s32[1,48,128]{2,1,0:T(8,128)}, u32[]{:S(2)}, u32[]{:S(2)}) collective-permute-start(s32[1,48,128]{2,1,0:T(8,128)} %get-tuple-element.95), channel_id=1, source_target_pairs={{0,4},{4,8},{8,12},{12,16},{16,20},{20,24},{24,28},{28,0},{1,5},{5... | collective-permute-start | bytes 73736 | tf_op jit(solution)/shard_map/ppermute | solution.py:44
  14.5 7.5 %collective-permute-start.1 = (s32[1,48,128]{2,1,0:T(8,128)}, s32[1,48,128]{2,1,0:T(8,128)}, u32[]{:S(2)}, u32[]{:S(2)}) collective-permute-start(s32[1,48,128]{2,1,0:T(8,128)} %get-tuple-element.94), channel_id=1, source_target_pairs={{4,0},{8,4},{12,8},{16,12},{20,16},{24,20},{28,24},{0,28},{5,1},{9... | collective-permute-start | bytes 73736 | tf_op jit(solution)/shard_map/ppermute | solution.py:46
  17.7 10.0 %collective-permute-start.5 = (f32[5,1,48,128]{3,2,1,0:T(8,128)}, f32[5,1,48,128]{3,2,1,0:T(8,128)}, u32[]{:S(2)}, u32[]{:S(2)}) collective-permute-start(f32[5,1,48,128]{3,2,1,0:T(8,128)} %get-tuple-element.40), channel_id=1, source_target_pairs={{0,28},{4,0},{8,4},{12,8},{16,12},{20,16},{24,20},{28,24},{1,29},{... | collective-permute-start | bytes 368648 | tf_op jit(solution)/shard_map/ppermute | solution.py:55
  22.8 1.5 %collective-permute-start.3 = (s32[5,1,128]{2,1,0:T(1,128)S(1)}, s32[5,1,128]{2,1,0:T(1,128)S(1)}, u32[]{:S(2)}, u32[]{:S(2)}) collective-permute-start(s32[5,1,128]{2,1,0:T(1,128)S(1)} %get-tuple-element.91), channel_id=1, source_target_pairs={{1,0},{2,1},{3,2},{0,3},{5,4},{6,5},{7,6},{4,7},{9,8},{10,9},{11,1... | collective-permute-start | bytes 7688 | tf_op jit(solution)/shard_map/ppermute | solution.py:46
  23.0 3.0 %collective-permute-start.2 = (s32[5,1,128]{2,1,0:T(1,128)S(1)}, s32[5,1,128]{2,1,0:T(1,128)S(1)}, u32[]{:S(2)}, u32[]{:S(2)}) collective-permute-start(s32[5,1,128]{2,1,0:T(1,128)S(1)} %get-tuple-element.90), channel_id=1, source_target_pairs={{0,1},{1,2},{2,3},{3,0},{4,5},{5,6},{6,7},{7,4},{8,9},{9,10},{10,1... | collective-permute-start | bytes 7688 | tf_op jit(solution)/shard_map/ppermute | solution.py:44
  26.2 2.3 %copy-start.2 = (f32[19,3,48,128]{3,2,1,0:T(8,128)S(1)}, f32[19,3,48,128]{3,2,1,0:T(8,128)}, u32[]{:S(2)}) copy-start(f32[19,3,48,128]{3,2,1,0:T(8,128)} %constant_dynamic-update-slice_fusion.41) | copy-start | bytes 4202500
  26.3 2.4 %copy-start.13 = (f32[2,48,128]{2,1,0:T(8,128)S(1)}, f32[2,48,128]{2,1,0:T(8,128)}, u32[]{:S(2)}) copy-start(f32[2,48,128]{2,1,0:T(8,128)} %get-tuple-element.28) | copy-start | bytes 147460
  26.5 4.3 %copy-start.10 = (f32[2,48,128]{2,1,0:T(8,128)S(1)}, f32[2,48,128]{2,1,0:T(8,128)}, u32[]{:S(2)}) copy-start(f32[2,48,128]{2,1,0:T(8,128)} %get-tuple-element.20) | copy-start | bytes 147460
  27.6 4.1 %copy-start.8 = (f32[2,48,128]{2,1,0:T(8,128)S(1)}, f32[2,48,128]{2,1,0:T(8,128)}, u32[]{:S(2)}) copy-start(f32[2,48,128]{2,1,0:T(8,128)} %get-tuple-element.25) | copy-start | bytes 147460
  27.6 4.1 %copy-start.7 = (f32[2,48,128]{2,1,0:T(8,128)S(1)}, f32[2,48,128]{2,1,0:T(8,128)}, u32[]{:S(2)}) copy-start(f32[2,48,128]{2,1,0:T(8,128)} %get-tuple-element.24) | copy-start | bytes 147460
  28.8 2.8 %collective-permute-start.6 = (f32[5,3,1,128]{3,2,1,0:T(1,128)S(1)}, f32[5,3,1,128]{3,2,1,0:T(1,128)S(1)}, u32[]{:S(2)}, u32[]{:S(2)}) collective-permute-start(f32[5,3,1,128]{3,2,1,0:T(1,128)S(1)} %constant_dynamic-update-slice_fusion.13), channel_id=1, source_target_pairs={{0,1},{1,2},{2,3},{4,5},{5,6},{6,7},{8,9},{9,10},{10,11},{12,13},{... | collective-permute-start | bytes 23048 | tf_op jit(solution)/shard_map/ppermute | solution.py:61
  31.7 4.2 %collective-permute-start.7 = (f32[5,3,1,128]{3,2,1,0:T(1,128)S(1)}, f32[5,3,1,128]{3,2,1,0:T(1,128)S(1)}, u32[]{:S(2)}, u32[]{:S(2)}) collective-permute-start(f32[5,3,1,128]{3,2,1,0:T(1,128)S(1)} %constant_dynamic-update-slice_fusion.18), channel_id=1, source_target_pairs={{1,0},{2,1},{3,2},{5,4},{6,5},{7,6},{9,8},{10,9},{11,10},{13,12},{... | collective-permute-start | bytes 23048 | tf_op jit(solution)/shard_map/ppermute | solution.py:61
  37.8 2.4 %copy-start.3 = (f32[19,3,48,128]{3,2,1,0:T(8,128)}, f32[19,3,48,128]{3,2,1,0:T(8,128)S(1)}, u32[]{:S(2)}) copy-start(f32[19,3,48,128]{3,2,1,0:T(8,128)S(1)} %get-tuple-element.7) | copy-start | bytes 4202500
  38.3 2.7 %copy-start.12 = (f32[3,48,128]{2,1,0:T(8,128)S(1)}, f32[3,48,128]{2,1,0:T(8,128)}, u32[]{:S(2)}) copy-start(f32[3,48,128]{2,1,0:T(8,128)} %multiply_select_fusion) | copy-start | bytes 221188
  38.3 2.7 %copy-start.21 = (f32[7]{0:T(128)S(1)}, f32[7]{0:T(128)}, u32[]{:S(2)}) copy-start(f32[7]{0:T(128)} %constant.16.clone) | copy-start | bytes 88
  41.3 5.7 %collective-permute-start.9 = (f32[7,1,48,128]{3,2,1,0:T(8,128)S(1)}, f32[7,1,48,128]{3,2,1,0:T(8,128)S(1)}, u32[]{:S(2)}, u32[]{:S(2)}) collective-permute-start(f32[7,1,48,128]{3,2,1,0:T(8,128)S(1)} %get-tuple-element.59), channel_id=1, source_target_pairs={{4,0},{8,4},{12,8},{16,12},{20,16},{24,20},{28,24},{0,28},{5,1},{9... | collective-permute-start | bytes 516104 | tf_op jit(solution)/shard_map/ppermute | solution.py:46
  44.0 8.3 %collective-permute-start.8 = (f32[7,1,48,128]{3,2,1,0:T(8,128)S(1)}, f32[7,1,48,128]{3,2,1,0:T(8,128)S(1)}, u32[]{:S(2)}, u32[]{:S(2)}) collective-permute-start(f32[7,1,48,128]{3,2,1,0:T(8,128)S(1)} %get-tuple-element.58), channel_id=1, source_target_pairs={{0,4},{4,8},{8,12},{12,16},{16,20},{20,24},{24,28},{28,0},{1,5},{5... | collective-permute-start | bytes 516104 | tf_op jit(solution)/shard_map/ppermute | solution.py:44
  52.3 3.2 %collective-permute-start.11 = (f32[7,5,1,128]{3,2,1,0:T(1,128)S(1)}, f32[7,5,1,128]{3,2,1,0:T(1,128)S(1)}, u32[]{:S(2)}, u32[]{:S(2)}) collective-permute-start(f32[7,5,1,128]{3,2,1,0:T(1,128)S(1)} %get-tuple-element.57), channel_id=1, source_target_pairs={{1,0},{2,1},{3,2},{0,3},{5,4},{6,5},{7,6},{4,7},{9,8},{10,9},{11,1... | collective-permute-start | bytes 53768 | tf_op jit(solution)/shard_map/ppermute | solution.py:46
  54.1 3.2 %collective-permute-start.10 = (f32[7,5,1,128]{3,2,1,0:T(1,128)S(1)}, f32[7,5,1,128]{3,2,1,0:T(1,128)S(1)}, u32[]{:S(2)}, u32[]{:S(2)}) collective-permute-start(f32[7,5,1,128]{3,2,1,0:T(1,128)S(1)} %get-tuple-element.56), channel_id=1, source_target_pairs={{0,1},{1,2},{2,3},{3,0},{4,5},{5,6},{6,7},{7,4},{8,9},{9,10},{10,1... | collective-permute-start | bytes 53768 | tf_op jit(solution)/shard_map/ppermute | solution.py:44
  (10 other events, 18.0 us)
where the time goes:
time: 59.3 us; the launch traced here: 58.8 us
  waiting for transfers between devices  17.5 us (30%)
  starting transfers between devices  16.4 us (28%)
  local copies, waits for them, and re-layouts  9.98 us (17%)
  other arithmetic  7.77 us (13%)
  matrix products  5.79 us (10%)
  between operations  1.36 us (2%)
    ppermute x4, waiting for transfers between devices, with_halo(): lax.ppermute(tail, axis, [(i, (i + 1) % count) for i in range(count)])  8.81 us
    ppermute x4, starting transfers between devices, with_halo(): lax.ppermute(head, axis, [((i + 1) % count, i) for i in range(count)])  7.88 us
    ppermute x4, waiting for transfers between devices, with_halo(): lax.ppermute(head, axis, [((i + 1) % count, i) for i in range(count)])  5.29 us
    unnamed x55, local copies, waits for them, and re-layouts  4.69 us
    dot_general x2, matrix products, moment(): jnp.tensordot(link_table.T, values, axes=1, precision=lax.Precision.HIGHEST)  3.42 us
    ppermute x2, waiting for transfers between devices, shifted(): return lax.ppermute(block, axis, route)  3.35 us
    ppermute x2, starting transfers between devices, shifted(): return lax.ppermute(block, axis, route)  3.32 us
    ppermute x2, starting transfers between devices, passed_along(): lax.ppermute(shard, axis, [(i, (i + by) % count) for i in range(count)])  3.31 us
  transfers between devices with their start and end apart: 12, of which 8 were waited for; matrix products, arithmetic and copies ran while one was open for 12% of the time, Pallas kernels for 0%

commit v1 on v0

v1 whole, which is shorter than its diff:
```python
import functools

import jax
import jax.numpy as jnp
import numpy as np
from jax import lax
from jax.experimental import pallas as pl
from jax.experimental.pallas import tpu as pltpu
from jax.sharding import PartitionSpec as P

LINKS19 = np.array(
    [
        [0, 0, 0],
        [1, 0, 0],
        [-1, 0, 0],
        [0, 1, 0],
        [0, -1, 0],
        [0, 0, 1],
        [0, 0, -1],
        [1, 1, 0],
        [-1, -1, 0],
        [1, -1, 0],
        [-1, 1, 0],
        [1, 0, 1],
        [-1, 0, -1],
        [1, 0, -1],
        [-1, 0, 1],
        [0, 1, 1],
        [0, -1, -1],
        [0, 1, -1],
        [0, -1, 1],
    ]
)
REVERSE19 = [0, 2, 1, 4, 3, 6, 5, 8, 7, 10, 9, 12, 11, 14, 13, 16, 15, 18, 17]
WEIGHTS19 = np.array([1.0 / 3.0] + [1.0 / 18.0] * 6 + [1.0 / 36.0] * 12)
WEIGHTS7 = np.array([0.25] + [0.125] * 6)
RELAX_FLOW = 1.25
RELAX_SOLUTE = 1.4


RISING = [d for d in range(19) if LINKS19[d][0] == 1]
FALLING = [d for d in range(19) if LINKS19[d][0] == -1]
ACROSS_UP = [d for d in range(19) if LINKS19[d][1] == 1]
ACROSS_DOWN = [d for d in range(19) if LINKS19[d][1] == -1]
CORNERS = [d for d in range(19) if LINKS19[d][0] != 0 and LINKS19[d][1] != 0]
TOP = 8
MESH = pl.DeviceIdType.MESH


def total(terms):
    terms = list(terms)
    while len(terms) > 1:
        terms = [sum(terms[i : i + 2][1:], terms[i]) for i in range(0, len(terms), 2)]
    return terms[0]


def momentum(values, axis):
    plus = total([values[d] for d in range(19) if LINKS19[d][axis] == 1])
    minus = total([values[d] for d in range(19) if LINKS19[d][axis] == -1])
    return plus - minus


def along(velocity, direction):
    parts = [(int(e), u) for e, u in zip(LINKS19[direction], velocity) if e != 0]
    sign, result = parts[0]
    result = result if sign == 1 else -result
    for sign, u in parts[1:]:
        result = result + u if sign == 1 else result - u
    return result


def kernel(
    pop_in, sol_in, mask_in, ids_in, rates, targets, flow_out, sol_out,
    pop, sol, mask, ids, relaxed, rock, carried,
    y_out, y_in, corner_out, corner_in, s_out, s_in,
    load_sem, store_sem, send_sem, recv_sem,
):
    _, depth, width, lanes = pop.shape
    last = depth - 1
    chunks = width // 8
    below_first, after_last = TOP - 1, TOP + width
    gz, gy = lax.axis_index("gz"), lax.axis_index("gy")
    nz, ny = lax.axis_size("gz"), lax.axis_size("gy")
    up, down = lax.rem(gz + 1, nz), lax.rem(gz + nz - 1, nz)
    right, left = lax.rem(gy + 1, ny), lax.rem(gy + ny - 1, ny)
    to_z = {1: up, 0: gz, -1: down}
    to_y = {1: right, 0: gy, -1: left}

    loads = [pltpu.make_async_copy(mask_in, mask, load_sem.at[0])]
    order = [0, last] + list(range(1, last))
    for k, p in enumerate(order):
        loads.append(
            pltpu.make_async_copy(pop_in.at[:, p], pop.at[:, p], load_sem.at[1 + k])
        )
    loads.append(pltpu.make_async_copy(sol_in, sol, load_sem.at[1 + depth]))
    loads.append(pltpu.make_async_copy(ids_in, ids, load_sem.at[2 + depth]))
    for copy in loads:
        copy.start()

    barrier = pltpu.get_barrier_semaphore()
    for ez in (1, 0, -1):
        for ey in (1, 0, -1):
            if (ez, ey) != (0, 0):
                pl.semaphore_signal(
                    barrier, inc=1, device_id=(to_z[ez], to_y[ey]), device_id_type=MESH
                )

    def remote(source, target, slot, ez, ey):
        return pltpu.make_async_remote_copy(
            src_ref=source,
            dst_ref=target,
            send_sem=send_sem.at[slot],
            recv_sem=recv_sem.at[slot],
            device_id=(to_z[ez], to_y[ey]),
            device_id_type=MESH,
        )

    inner = pl.ds(TOP, width)

    loads[0].wait()
    for p in range(depth):
        rock[p + 1, TOP : TOP + width] = mask[p].astype(jnp.float32)

    def relax(p):
        def step(c, _):
            rows = pl.ds(pl.multiple_of(c * 8, 8), 8)
            spread = pl.ds(pl.multiple_of(c * 8 + TOP, 8), 8)
            f = [pop[d, p, rows] for d in range(19)]
            density = total(f)
            inverse = 1.0 / density
            velocity = [momentum(f, axis) * inverse for axis in range(3)]
            speed = total([u * u for u in velocity])
            share = 1.0 / RELAX_FLOW
            rest = 1.0 - 1.5 * speed
            scaled = {w: density * float(share * w) for w in sorted(set(WEIGHTS19))}
            relaxed[0, p + 1, spread] = (1.0 - share) * f[0] + scaled[WEIGHTS19[0]] * rest
            for d in range(1, 19, 2):
                projected = along(velocity, d)
                even = rest + 4.5 * projected * projected
                odd = 3.0 * projected
                weight = scaled[WEIGHTS19[d]]
                relaxed[d, p + 1, spread] = (1.0 - share) * f[d] + weight * (even + odd)
                relaxed[d + 1, p + 1, spread] = (1.0 - share) * f[d + 1] + weight * (even - odd)
            return 0

        lax.fori_loop(0, chunks, step, 0)

    loads[1].wait()
    relax(0)
    loads[2].wait()
    relax(last)
    first_row, end_row = TOP, TOP + width - 1
    for k, d in enumerate(CORNERS):
        p = depth if LINKS19[d][0] == 1 else 1
        r = end_row if LINKS19[d][1] == 1 else first_row
        corner_out[k, 0:1] = relaxed[d, p, r : r + 1]
        corner_out[k, 1:2] = rock[p, r : r + 1]

    pl.semaphore_wait(barrier, 8)
    to_up = [remote(rock.at[depth, inner], rock.at[0, inner], 0, 1, 0)]
    to_down = [remote(rock.at[1, inner], rock.at[depth + 1, inner], 1, -1, 0)]
    for k, (d, e) in enumerate(zip(RISING, FALLING)):
        to_up.append(
            remote(relaxed.at[d, depth, inner], relaxed.at[d, 0, inner], 2 + 2 * k, 1, 0)
        )
        to_down.append(
            remote(relaxed.at[e, 1, inner], relaxed.at[e, depth + 1, inner], 3 + 2 * k, -1, 0)
        )
    corners = [
        remote(
            corner_out.at[k], corner_in.at[k], 12 + k, int(LINKS19[d][0]), int(LINKS19[d][1])
        )
        for k, d in enumerate(CORNERS)
    ]
    for copy in corners:
        copy.start()
    for a, b in zip(to_up, to_down):
        a.start()
        b.start()

    for k in range(2, depth):
        loads[1 + k].wait()
    lax.fori_loop(1, last, lambda p, _: (relax(p), 0)[1], 0)
    for side, links, r in ((0, ACROSS_UP, end_row), (1, ACROSS_DOWN, first_row)):
        for k, d in enumerate(links):
            for p in range(depth):
                row = k * depth + p
                y_out[side, row : row + 1] = relaxed[d, p + 1, r : r + 1]
        for p in range(depth):
            row = 5 * depth + p
            y_out[side, row : row + 1] = rock[p + 1, r : r + 1]
    y_copies = [
        remote(y_out.at[0], y_in.at[0], 16, 0, 1),
        remote(y_out.at[1], y_in.at[1], 17, 0, -1),
    ]
    for copy in y_copies:
        copy.start()
    loads[1 + depth].wait()
    loads[2 + depth].wait()
    for copy in y_copies:
        copy.wait_recv()
    open_side = [
        jnp.where(gy == 0, 0.0, 1.0),
        jnp.where(gy == ny - 1, 0.0, 1.0),
    ]
    for side, links, r in ((0, ACROSS_UP, below_first), (1, ACROSS_DOWN, after_last)):
        for k, d in enumerate(links):
            for p in range(depth):
                row = k * depth + p
                relaxed[d, p + 1, r : r + 1] = y_in[side, row : row + 1]
        for p in range(depth):
            row = 5 * depth + p
            rock[p + 1, r : r + 1] = y_in[side, row : row + 1] * open_side[side]

    def source_rock(direction, p, c):
        ez, ey, ex = (int(v) for v in LINKS19[direction])
        found = rock[p + 1 - ez, pl.ds(TOP - ey + c * 8, 8)]
        return found if ex == 0 else pltpu.roll(found, ex % lanes, 1)

    def pulled(store, direction, p, c):
        ez, ey, ex = (int(v) for v in LINKS19[direction])
        found = store[direction, p + 1 - ez, pl.ds(TOP - ey + c * 8, 8)]
        return found if ex == 0 else pltpu.roll(found, ex % lanes, 1)

    def flow_rows(p, c):
        rows = pl.ds(c * 8, 8)
        spread = pl.ds(c * 8 + TOP, 8)
        here = mask[p, rows]
        solid = here == 0
        flow = []
        for d in range(19):
            if d == 0:
                passed = relaxed[0, p + 1, spread]
            else:
                passed = jnp.where(
                    source_rock(d, p, c) == 0.0,
                    relaxed[REVERSE19[d], p + 1, spread],
                    pulled(relaxed, d, p, c),
                )
            value = jnp.where(solid, pop[d, p, rows], passed)
            pop[d, p, rows] = value
            flow.append(value)
        inverse = jnp.where(solid, 0.0, 1.0 / total(flow))
        velocity = [momentum(flow, axis) * inverse for axis in range(3)]
        s = [sol[d, p, rows] for d in range(7)]
        concentration = total(s)
        kind = ids[p, rows]
        rate = jnp.zeros_like(concentration)
        target = jnp.zeros_like(concentration)
        for k in range(rates.shape[0]):
            chosen = kind == k
            rate = jnp.where(chosen, rates[k], rate)
            target = jnp.where(chosen, targets[k], target)
        reaction = jnp.where(here == 2, rate * (target - concentration), 0.0)
        share = 1.0 / RELAX_SOLUTE
        for weight, links in ((0.25, (0,)), (0.125, range(1, 7))):
            level = weight * (share * concentration + reaction)
            slope = (4.0 * share * weight) * concentration
            for d in links:
                value = (1.0 - share) * s[d] + level
                if d:
                    value = value + slope * along(velocity, d)
                carried[d, p + 1, spread] = value

    def solute_rows(p, c):
        rows = pl.ds(c * 8, 8)
        spread = pl.ds(c * 8 + TOP, 8)
        solid = mask[p, rows] == 0
        for d in range(7):
            if d == 0:
                passed = carried[0, p + 1, spread]
            else:
                passed = jnp.where(
                    source_rock(d, p, c) == 0.0,
                    carried[REVERSE19[d], p + 1, spread],
                    pulled(carried, d, p, c),
                )
            sol[d, p, rows] = jnp.where(solid, sol[d, p, rows], passed)

    def plane(rows_of, p):
        for c in range(chunks):
            rows_of(p, c)

    stores = []

    def store(source, target, p):
        copy = pltpu.make_async_copy(source.at[:, p], target.at[:, p], store_sem.at[len(stores)])
        copy.start()
        stores.append(copy)

    lax.fori_loop(1, last, lambda p, _: (plane(flow_rows, p), 0)[1], 0)
    for p in range(1, last):
        store(pop, flow_out, p)

    for copy in corners:
        copy.wait_recv()
    for k, d in enumerate(CORNERS):
        p = 0 if LINKS19[d][0] == 1 else depth + 1
        side, r = (0, below_first) if LINKS19[d][1] == 1 else (1, after_last)
        relaxed[d, p, r : r + 1] = corner_in[k, 0:1]
        rock[p, r : r + 1] = corner_in[k, 1:2] * open_side[side]

    s_up = remote(carried.at[1, depth, inner], carried.at[1, 0, inner], 18, 1, 0)
    s_down = remote(carried.at[2, 1, inner], carried.at[2, depth + 1, inner], 19, -1, 0)
    for copy in to_up:
        copy.wait_recv()
    plane(flow_rows, 0)
    s_down.start()
    store(pop, flow_out, 0)
    for copy in to_down:
        copy.wait_recv()
    plane(flow_rows, last)
    s_up.start()
    store(pop, flow_out, last)

    for side, d, r in ((0, 3, end_row), (1, 4, first_row)):
        for p in range(depth):
            s_out[side, p : p + 1] = carried[d, p + 1, r : r + 1]
    s_copies = [
        remote(s_out.at[0], s_in.at[0], 20, 0, 1),
        remote(s_out.at[1], s_in.at[1], 21, 0, -1),
    ]
    for copy in s_copies:
        copy.start()
    for copy in s_copies:
        copy.wait_recv()
    for side, d, r in ((0, 3, below_first), (1, 4, after_last)):
        for p in range(depth):
            carried[d, p + 1, r : r + 1] = s_in[side, p : p + 1]
    lax.fori_loop(1, last, lambda p, _: (plane(solute_rows, p), 0)[1], 0)
    for p in range(1, last):
        store(sol, sol_out, p)
    s_up.wait_recv()
    plane(solute_rows, 0)
    store(sol, sol_out, 0)
    s_down.wait_recv()
    plane(solute_rows, last)
    store(sol, sol_out, last)

    for copy in to_up + to_down + corners + y_copies + s_copies + [s_up, s_down]:
        copy.wait_send()
    for copy in stores:
        copy.wait()


def on_device(populations, solute, pore_mask, mineral_ids, reaction_rates, saturation):
    depth, width, lanes = pore_mask.shape
    rows = TOP + width + 8
    f32 = jnp.float32
    y_rows = -(-6 * depth // 8) * 8
    s_rows = -(-depth // 8) * 8
    anywhere = pl.BlockSpec(memory_space=pl.ANY)
    scalars = pl.BlockSpec(memory_space=pltpu.SMEM)
    return tuple(
        pl.pallas_call(
            kernel,
            out_shape=(
                jax.ShapeDtypeStruct(populations.shape, f32),
                jax.ShapeDtypeStruct(solute.shape, f32),
            ),
            in_specs=[anywhere] * 4 + [scalars] * 2,
            out_specs=(anywhere, anywhere),
            scratch_shapes=[
                pltpu.VMEM(populations.shape, f32),
                pltpu.VMEM(solute.shape, f32),
                pltpu.VMEM(pore_mask.shape, jnp.int32),
                pltpu.VMEM(mineral_ids.shape, jnp.int32),
                pltpu.VMEM((19, depth + 2, rows, lanes), f32),
                pltpu.VMEM((depth + 2, rows, lanes), f32),
                pltpu.VMEM((7, depth + 2, rows, lanes), f32),
                pltpu.VMEM((2, y_rows, lanes), f32),
                pltpu.VMEM((2, y_rows, lanes), f32),
                pltpu.VMEM((4, 8, lanes), f32),
                pltpu.VMEM((4, 8, lanes), f32),
                pltpu.VMEM((2, s_rows, lanes), f32),
                pltpu.VMEM((2, s_rows, lanes), f32),
                pltpu.SemaphoreType.DMA((depth + 3,)),
                pltpu.SemaphoreType.DMA((2 * depth,)),
                pltpu.SemaphoreType.DMA((22,)),
                pltpu.SemaphoreType.DMA((22,)),
            ],
            compiler_params=pltpu.CompilerParams(collective_id=0, has_side_effects=True),
        )(populations, solute, pore_mask, mineral_ids, reaction_rates, saturation)
    )


def solution(mesh):
    return jax.shard_map(
        on_device,
        mesh=mesh,
        in_specs=(
            P(None, "gz", "gy", None),
            P(None, "gz", "gy", None),
            P("gz", "gy", None),
            P("gz", "gy", None),
            P(),
            P(),
        ),
        out_specs=(P(None, "gz", "gy", None), P(None, "gz", "gy", None)),
        check_vma=False,
    )
```

time: 59.3 us -> 25.3 us (0.43)
  Pallas kernels: 0 us -> 21.1 us
  waiting for transfers between devices: 17.5 us -> 0 us
  starting transfers between devices: 16.4 us -> 0 us
  other arithmetic: 7.77 us -> 0 us
  local copies, waits for them, and re-layouts: 9.98 us -> 3.37 us
  matrix products: 5.79 us -> 0 us
  between operations: 1.36 us -> 0.65 us
    pallas_call x0 -> x1, Pallas kernels: none -> 21.1 us  [on_device(): pl.pallas_call(kernel, out_shape=(jax.ShapeDtypeStruct(populations.shape,...]
    ppermute x12 -> x0, waiting for transfers between devices: 17.5 us -> none  [the longest x4 8.81 us: with_halo(): lax.ppermute(tail, axis, [(i, (i + 1) % count) for i in range(count)])]
    ppermute x12 -> x0, starting transfers between devices: 16.4 us -> none  [the longest x4 7.88 us: with_halo(): lax.ppermute(head, axis, [((i + 1) % count, i) for i in range(count)])]
    dot_general x4 -> x0, matrix products: 5.79 us -> none  [the longest x2 3.42 us: moment(): jnp.tensordot(link_table.T, values, axes=1, precision=lax.Precision.HIGHEST)]
    reduce_sum x4 -> x0, other arithmetic: 2.84 us -> none  [the longest x1 1.54 us: on_device(): density = jnp.sum(populations, 0)]
    squeeze x5 -> x0, local copies, waits for them, and re-layouts: 2.55 us -> none  [the longest x1 0.93 us: on_device(): lower_planes[rising.index(direction)]]
    select_n x3 -> x0, other arithmetic: 1.59 us -> none  [the longest x1 0.86 us: on_device(): jnp.where(pore_mask[None] == 0, solute, jnp.stack(solute_moved))]
    concatenate x9 -> x0, local copies, waits for them, and re-layouts: 1.42 us -> none  [the longest x1 0.74 us: with_halo(): jnp.concatenate([lax.ppermute(tail, axis, [(i, (i + 1) % count) for i in...]
  transfers between devices with their start and end apart: 12 -> 0, of which waited for: 8 -> 0; matrix products, arithmetic and copies ran while one was open for 12% -> 0% of each run, Pallas kernels for 0% -> 0%
where the time goes in v1:
time: 25.3 us; the launch traced here: 25.1 us
  Pallas kernels  21.1 us (83%)
  local copies, waits for them, and re-layouts  3.37 us (13%)
  between operations  0.65 us (3%)
    pallas_call x1, Pallas kernels, on_device(): pl.pallas_call(kernel, out_shape=(jax.ShapeDtypeStruct(populations.shape,...  21.1 us
    unnamed x4, local copies, waits for them, and re-layouts  3.37 us

profile of v1, /device:TPU:0, one launch (start us, length us, event | category | flops | bytes accessed | tf_op | source)
XLA Modules:
  0.0 25.1 jit_solution(1518984511878578477)
XLA Ops:
  0.6 21.1 %shard_map.77 = (f32[19,3,48,128]{3,2,1,0:T(8,128)}, f32[7,3,48,128]{3,2,1,0:T(8,128)}) custom-call(f32[19,3,48,128]{3,2,1,0:T(8,128)} %pop_in.1, f32[7,3,48,128]{3,2,1,0:T(8,128)} %sol_in.1, s32[3,48,128]{2,1,0:T(8,128)} %mask_in.1, s32[3,48,128]{2,1,0:T(8,128)} %ids_in.1, f32[8]{0:T(128)} %rates.1, f32[8]{0:T(128)} %targets.1), custom_call_target="tpu_custom_call" | custom-call | tf_op jit(solution)/shard_map/pallas_call | solution.py:355
  21.7 0.0 copy-start
  21.7 2.6 %copy.10 = f32[19,3,48,128]{3,2,1,0:T(8,128)} copy(f32[19,3,48,128]{3,2,1,0:T(8,128)} %get-tuple-element.4) | data formatting | bytes 2801664
  24.3 0.0 copy-done
  24.3 0.8 %copy.11 = f32[7,3,48,128]{3,2,1,0:T(8,128)} copy(f32[7,3,48,128]{3,2,1,0:T(8,128)S(1)} %copy-done) | data formatting | bytes 1032192
Async XLA Ops:
  21.7 2.6 %copy-start = (f32[7,3,48,128]{3,2,1,0:T(8,128)S(1)}, f32[7,3,48,128]{3,2,1,0:T(8,128)}, u32[]{:S(2)}) copy-start(f32[7,3,48,128]{3,2,1,0:T(8,128)} %get-tuple-element.5) | copy-start | bytes 1548292

commit v2 on v1

--- a/solution.py
+++ b/solution.py
@@ -69,11 +69,23 @@
     return result
 
 
+def source_rock(rock, direction, p, c):
+    ez, ey, ex = (int(v) for v in LINKS19[direction])
+    found = rock[p + 1 - ez, pl.ds(TOP - ey + c * 8, 8)]
+    return found if ex == 0 else pltpu.roll(found, ex % rock.shape[-1], 1)
+
+
+def pulled(store, direction, p, c):
+    ez, ey, ex = (int(v) for v in LINKS19[direction])
+    found = store[direction, p + 1 - ez, pl.ds(TOP - ey + c * 8, 8)]
+    return found if ex == 0 else pltpu.roll(found, ex % store.shape[-1], 1)
+
+
 def kernel(
-    pop_in, sol_in, mask_in, ids_in, rates, targets, flow_out, sol_out,
-    pop, sol, mask, ids, relaxed, rock, carried,
+    pop_in, sol_in, mask_in, ids_in, rates, targets,
+    pop, sol, carried, rock, mask, ids, relaxed,
     y_out, y_in, corner_out, corner_in, s_out, s_in,
-    load_sem, store_sem, send_sem, recv_sem,
+    load_sem, send_sem, recv_sem,
 ):
     _, depth, width, lanes = pop.shape
     last = depth - 1
@@ -212,16 +224,6 @@
             row = 5 * depth + p
             rock[p + 1, r : r + 1] = y_in[side, row : row + 1] * open_side[side]
 
-    def source_rock(direction, p, c):
-        ez, ey, ex = (int(v) for v in LINKS19[direction])
-        found = rock[p + 1 - ez, pl.ds(TOP - ey + c * 8, 8)]
-        return found if ex == 0 else pltpu.roll(found, ex % lanes, 1)
-
-    def pulled(store, direction, p, c):
-        ez, ey, ex = (int(v) for v in LINKS19[direction])
-        found = store[direction, p + 1 - ez, pl.ds(TOP - ey + c * 8, 8)]
-        return found if ex == 0 else pltpu.roll(found, ex % lanes, 1)
-
     def flow_rows(p, c):
         rows = pl.ds(c * 8, 8)
         spread = pl.ds(c * 8 + TOP, 8)
@@ -233,7 +235,7 @@
                 passed = relaxed[0, p + 1, spread]
             else:
                 passed = jnp.where(
-                    source_rock(d, p, c) == 0.0,
+                    source_rock(rock, d, p, c) == 0.0,
                     relaxed[REVERSE19[d], p + 1, spread],
                     pulled(relaxed, d, p, c),
                 )
@@ -262,35 +264,11 @@
                     value = value + slope * along(velocity, d)
                 carried[d, p + 1, spread] = value
 
-    def solute_rows(p, c):
-        rows = pl.ds(c * 8, 8)
-        spread = pl.ds(c * 8 + TOP, 8)
-        solid = mask[p, rows] == 0
-        for d in range(7):
-            if d == 0:
-                passed = carried[0, p + 1, spread]
-            else:
-                passed = jnp.where(
-                    source_rock(d, p, c) == 0.0,
-                    carried[REVERSE19[d], p + 1, spread],
-                    pulled(carried, d, p, c),
-                )
-            sol[d, p, rows] = jnp.where(solid, sol[d, p, rows], passed)
-
-    def plane(rows_of, p):
+    def plane(p):
         for c in range(chunks):
-            rows_of(p, c)
-
-    stores = []
-
-    def store(source, target, p):
-        copy = pltpu.make_async_copy(source.at[:, p], target.at[:, p], store_sem.at[len(stores)])
-        copy.start()
-        stores.append(copy)
-
-    lax.fori_loop(1, last, lambda p, _: (plane(flow_rows, p), 0)[1], 0)
-    for p in range(1, last):
-        store(pop, flow_out, p)
+            flow_rows(p, c)
+
+    lax.fori_loop(1, last, lambda p, _: (plane(p), 0)[1], 0)
 
     for copy in corners:
         copy.wait_recv()
@@ -304,14 +282,12 @@
     s_down = remote(carried.at[2, 1, inner], carried.at[2, depth + 1, inner], 19, -1, 0)
     for copy in to_up:
         copy.wait_recv()
-    plane(flow_rows, 0)
+    plane(0)
     s_down.start()
-    store(pop, flow_out, 0)
     for copy in to_down:
         copy.wait_recv()
-    plane(flow_rows, last)
+    plane(last)
     s_up.start()
-    store(pop, flow_out, last)
 
     for side, d, r in ((0, 3, end_row), (1, 4, first_row)):
         for p in range(depth):
@@ -327,18 +303,36 @@
     for side, d, r in ((0, 3, below_first), (1, 4, after_last)):
         for p in range(depth):
             carried[d, p + 1, r : r + 1] = s_in[side, p : p + 1]
-    lax.fori_loop(1, last, lambda p, _: (plane(solute_rows, p), 0)[1], 0)
-    for p in range(1, last):
-        store(sol, sol_out, p)
     s_up.wait_recv()
-    plane(solute_rows, 0)
-    store(sol, sol_out, 0)
     s_down.wait_recv()
-    plane(solute_rows, last)
-    store(sol, sol_out, last)
-
     for copy in to_up + to_down + corners + y_copies + s_copies + [s_up, s_down]:
         copy.wait_send()
+
+
+def finish(flow, sol, carried, rock, flow_out, sol_out, moved, store_sem):
+    _, depth, width, lanes = sol.shape
+    stores = [pltpu.make_async_copy(flow, flow_out, store_sem.at[0])]
+    stores[0].start()
+
+    for p in range(depth):
+        for c in range(width // 8):
+            rows = pl.ds(c * 8, 8)
+            spread = pl.ds(c * 8 + TOP, 8)
+            solid = rock[p + 1, spread] == 0.0
+            for d in range(7):
+                if d == 0:
+                    passed = carried[0, p + 1, spread]
+                else:
+                    passed = jnp.where(
+                        source_rock(rock, d, p, c) == 0.0,
+                        carried[REVERSE19[d], p + 1, spread],
+                        pulled(carried, d, p, c),
+                    )
+                moved[d, p, rows] = jnp.where(solid, sol[d, p, rows], passed)
+        stores.append(
+            pltpu.make_async_copy(moved.at[:, p], sol_out.at[:, p], store_sem.at[1 + p])
+        )
+        stores[-1].start()
     for copy in stores:
         copy.wait()
 
@@ -349,38 +343,52 @@
     f32 = jnp.float32
     y_rows = -(-6 * depth // 8) * 8
     s_rows = -(-depth // 8) * 8
-    anywhere = pl.BlockSpec(memory_space=pl.ANY)
+    anywhere = pl.BlockSpec(memory_space=pltpu.HBM)
     scalars = pl.BlockSpec(memory_space=pltpu.SMEM)
+    inside = pl.BlockSpec(memory_space=pltpu.VMEM)
+    held = pl.pallas_call(
+        kernel,
+        out_shape=(
+            pltpu.VMEM(populations.shape, f32),
+            pltpu.VMEM(solute.shape, f32),
+            pltpu.VMEM((7, depth + 2, rows, lanes), f32),
+            pltpu.VMEM((depth + 2, rows, lanes), f32),
+        ),
+        in_specs=[anywhere] * 4 + [scalars] * 2,
+        out_specs=(inside,) * 4,
+        scratch_shapes=[
+            pltpu.VMEM(pore_mask.shape, jnp.int32),
+            pltpu.VMEM(mineral_ids.shape, jnp.int32),
+            pltpu.VMEM((19, depth + 2, rows, lanes), f32),
+            pltpu.VMEM((2, y_rows, lanes), f32),
+            pltpu.VMEM((2, y_rows, lanes), f32),
+            pltpu.VMEM((4, 8, lanes), f32),
+            pltpu.VMEM((4, 8, lanes), f32),
+            pltpu.VMEM((2, s_rows, lanes), f32),
+            pltpu.VMEM((2, s_rows, lanes), f32),
+            pltpu.SemaphoreType.DMA((depth + 3,)),
+            pltpu.SemaphoreType.DMA((22,)),
+            pltpu.SemaphoreType.DMA((22,)),
+        ],
+        compiler_params=pltpu.CompilerParams(
+            collective_id=0, has_side_effects=True, vmem_limit_bytes=24 * 2**20
+        ),
+    )(populations, solute, pore_mask, mineral_ids, reaction_rates, saturation)
     return tuple(
         pl.pallas_call(
-            kernel,
+            finish,
             out_shape=(
                 jax.ShapeDtypeStruct(populations.shape, f32),
                 jax.ShapeDtypeStruct(solute.shape, f32),
             ),
-            in_specs=[anywhere] * 4 + [scalars] * 2,
+            in_specs=[inside] * 4,
             out_specs=(anywhere, anywhere),
             scratch_shapes=[
-                pltpu.VMEM(populations.shape, f32),
                 pltpu.VMEM(solute.shape, f32),
-                pltpu.VMEM(pore_mask.shape, jnp.int32),
-                pltpu.VMEM(mineral_ids.shape, jnp.int32),
-                pltpu.VMEM((19, depth + 2, rows, lanes), f32),
-                pltpu.VMEM((depth + 2, rows, lanes), f32),
-                pltpu.VMEM((7, depth + 2, rows, lanes), f32),
-                pltpu.VMEM((2, y_rows, lanes), f32),
-                pltpu.VMEM((2, y_rows, lanes), f32),
-                pltpu.VMEM((4, 8, lanes), f32),
-                pltpu.VMEM((4, 8, lanes), f32),
-                pltpu.VMEM((2, s_rows, lanes), f32),
-                pltpu.VMEM((2, s_rows, lanes), f32),
-                pltpu.SemaphoreType.DMA((depth + 3,)),
-                pltpu.SemaphoreType.DMA((2 * depth,)),
-                pltpu.SemaphoreType.DMA((22,)),
-                pltpu.SemaphoreType.DMA((22,)),
+                pltpu.SemaphoreType.DMA((depth + 1,)),
             ],
-            compiler_params=pltpu.CompilerParams(collective_id=0, has_side_effects=True),
-        )(populations, solute, pore_mask, mineral_ids, reaction_rates, saturation)
+            compiler_params=pltpu.CompilerParams(vmem_limit_bytes=24 * 2**20),
+        )(*held)
     )
 
 

time: 25.3 us -> 28.3 us (1.12)
  local copies, waits for them, and re-layouts: 3.37 us -> 5.46 us
  Pallas kernels: 21.1 us -> 21.9 us
    unnamed x4 -> x12, local copies, waits for them, and re-layouts: 3.37 us -> 5.46 us
    pallas_call x1 -> x2, Pallas kernels: 21.1 us -> 21.9 us  [the longest x1 20.6 us: on_device(): pl.pallas_call(kernel, out_shape=(pltpu.VMEM(populations.shape, f32), plt...]
where the time goes in v2:
time: 28.3 us; the launch traced here: 28 us
  Pallas kernels  21.9 us (77%)
  local copies, waits for them, and re-layouts  5.46 us (19%)
  between operations  0.65 us (2%)
    pallas_call x1, Pallas kernels, on_device(): pl.pallas_call(kernel, out_shape=(pltpu.VMEM(populations.shape, f32), plt...  20.6 us
    unnamed x12, local copies, waits for them, and re-layouts  5.46 us
    pallas_call x1, Pallas kernels, on_device(): pl.pallas_call(finish, out_shape=(jax.ShapeDtypeStruct(populations.shape,...  1.28 us

profile of v2, /device:TPU:0, one launch (start us, length us, event | category | flops | bytes accessed | tf_op | source)
XLA Modules:
  0.0 28.0 jit_solution(13550769418926961060)
XLA Ops:
  0.6 0.0 copy-start
  0.6 1.3 %copy-done = f32[19,3,48,128]{3,2,1,0:T(8,128)S(1)} copy-done((f32[19,3,48,128]{3,2,1,0:T(8,128)S(1)}, f32[19,3,48,128]{3,2,1,0:T(8,128)}, u32[]{:S(2)}) %copy-start) | copy-done | bytes 1400856
  2.0 0.0 copy-start.1
  2.0 1.0 %copy-done.1 = f32[7,3,48,128]{3,2,1,0:T(8,128)S(1)} copy-done((f32[7,3,48,128]{3,2,1,0:T(8,128)S(1)}, f32[7,3,48,128]{3,2,1,0:T(8,128)}, u32[]{:S(2)}) %copy-start.1) | copy-done | bytes 516120
  3.0 0.0 copy-start.2
  3.0 0.9 %copy-done.2 = s32[3,48,128]{2,1,0:T(8,128)S(1)} copy-done((s32[3,48,128]{2,1,0:T(8,128)S(1)}, s32[3,48,128]{2,1,0:T(8,128)}, u32[]{:S(2)}) %copy-start.2) | copy-done | bytes 73752
  3.9 0.0 copy-start.3
  3.9 0.9 %copy-done.3 = s32[3,48,128]{2,1,0:T(8,128)S(1)} copy-done((s32[3,48,128]{2,1,0:T(8,128)S(1)}, s32[3,48,128]{2,1,0:T(8,128)}, u32[]{:S(2)}) %copy-start.3) | copy-done | bytes 73752
  4.8 0.0 copy-start.4
  4.8 0.7 %copy-done.4 = f32[8]{0:T(128)S(1)} copy-done((f32[8]{0:T(128)S(1)}, f32[8]{0:T(128)}, u32[]{:S(2)}) %copy-start.4) | copy-done | bytes 56
  5.4 0.0 copy-start.5
  5.4 0.7 %copy-done.5 = f32[8]{0:T(128)S(1)} copy-done((f32[8]{0:T(128)S(1)}, f32[8]{0:T(128)}, u32[]{:S(2)}) %copy-start.5) | copy-done | bytes 56
  6.1 20.6 %shard_map.77 = (f32[19,3,48,128]{3,2,1,0:T(8,128)S(1)}, f32[7,3,48,128]{3,2,1,0:T(8,128)S(1)}, f32[7,5,64,128]{3,2,1,0:T(8,128)S(1)}, f32[5,64,128]{2,1,0:T(8,128)S(1)}) custom-call(f32[19,3,48,128]{3,2,1,0:T(8,128)S(1)} %copy-done, f32[7,3,48,128]{3,2,1,0:T(8,128)S(1)} %copy-done.1, s32[3,48,128]{2,1,0:T(8,128)S(1)} %copy-done.2, ...), custom_call_target="tpu_custom_call" | custom-call | tf_op jit(solution)/shard_map/pallas_call | solution.py:349
  26.8 1.3 %shard_map.78 = (f32[19,3,48,128]{3,2,1,0:T(8,128)}, f32[7,3,48,128]{3,2,1,0:T(8,128)}) custom-call(f32[19,3,48,128]{3,2,1,0:T(8,128)S(1)} %get-tuple-element.6.flow, f32[7,3,48,128]{3,2,1,0:T(8,128)S(1)} %get-tuple-element.7.sol, f32[7,5,64,128]{3,2,1,0:T(8,128)S(1)} %get-tuple-element.8.carried, f32[5,64,128]{2,1,0:T(8,128)S(1)} %get-tuple-element.9.rock), custom_call_target="tpu_custom_call" | custom-call | tf_op jit(solution)/shard_map/pallas_call | solution.py:378
Async XLA Ops:
  0.6 1.3 %copy-start = (f32[19,3,48,128]{3,2,1,0:T(8,128)S(1)}, f32[19,3,48,128]{3,2,1,0:T(8,128)}, u32[]{:S(2)}) copy-start(f32[19,3,48,128]{3,2,1,0:T(8,128)} %pop_in.1) | copy-start | bytes 4202500
  2.0 1.0 %copy-start.1 = (f32[7,3,48,128]{3,2,1,0:T(8,128)S(1)}, f32[7,3,48,128]{3,2,1,0:T(8,128)}, u32[]{:S(2)}) copy-start(f32[7,3,48,128]{3,2,1,0:T(8,128)} %sol_in.1) | copy-start | bytes 1548292
  3.0 0.9 %copy-start.2 = (s32[3,48,128]{2,1,0:T(8,128)S(1)}, s32[3,48,128]{2,1,0:T(8,128)}, u32[]{:S(2)}) copy-start(s32[3,48,128]{2,1,0:T(8,128)} %mask_in.1) | copy-start | bytes 221188
  3.9 0.9 %copy-start.3 = (s32[3,48,128]{2,1,0:T(8,128)S(1)}, s32[3,48,128]{2,1,0:T(8,128)}, u32[]{:S(2)}) copy-start(s32[3,48,128]{2,1,0:T(8,128)} %ids_in.1) | copy-start | bytes 221188
  4.8 0.7 %copy-start.4 = (f32[8]{0:T(128)S(1)}, f32[8]{0:T(128)}, u32[]{:S(2)}) copy-start(f32[8]{0:T(128)} %rates.1) | copy-start | bytes 100
  5.4 0.7 %copy-start.5 = (f32[8]{0:T(128)S(1)}, f32[8]{0:T(128)}, u32[]{:S(2)}) copy-start(f32[8]{0:T(128)} %targets.1) | copy-start | bytes 100
